TPU v7x, 128 devices: a whole 4x4x4 slice. The times are simulated.
128 devices in a mesh: tp: 16 (over x_lo, z, core), seq: 8 (over y, x_hi).
Axes of the slice: x: 4 (x_hi: 2, x_lo: 2; x = x_hi * 2 + x_lo), y: 4, z: 4, core: 2. Of those that a mesh axis runs over, the one named last changes fastest.
Arguments:
- residual: bfloat16 [2048, 4096], P('seq'), may hold values from -6 to 6
- mix_gain: float32 [4096], replicated, may hold values from 0.5 to 1.5
- in_proj: bfloat16 [4096, 4096], P(None, 'tp'), may hold values from -0.09375 to 0.09375
- branch_proj: bfloat16 [4096, 4096], P(None, 'tp'), may hold values from -0.09375 to 0.09375
- conv_weight: float32 [4, 4096], P(None, 'tp'), may hold values from -3 to 3
- conv_bias: float32 [4096], P('tp'), may hold values from -1.25 to 1.25
- input_gate: bfloat16 [16, 256, 256], P('tp'), may hold values from -0.375 to 0.375
- input_bias: float32 [4096], P('tp'), may hold values from -3 to 3
- decay_gate: bfloat16 [16, 256, 256], P('tp'), may hold values from -0.375 to 0.375
- decay_bias: float32 [4096], P('tp'), may hold values from -3 to 3
- decay_param: float32 [4096], P('tp'), may hold values from -13 to -2, as said below
- out_proj: bfloat16 [4096, 4096], P('tp'), may hold values from -0.25 to 0.25
- mlp_gain: float32 [4096], replicated, may hold values from 0.5 to 1.5
- gate_proj: bfloat16 [4096, 12288], P('seq', 'tp'), may hold values from -0.09375 to 0.09375
- up_proj: bfloat16 [4096, 12288], P('seq', 'tp'), may hold values from -0.09375 to 0.09375
- down_proj: bfloat16 [12288, 4096], P('tp'), may hold values from -0.078125 to 0.078125
Outputs:
- updated: bfloat16 [2048, 4096], P('seq')
Inputs may be any that keep to these rules, and one draw needn't show every extreme that they name: softplus(decay_param) lies between 0.02 / 2048 and 0.1 for every channel.
All inputs are finite; a program needn't handle non-finite values.
Results may differ from a plain program's by a relative error of at most 0.02.
Values may be sent and summed in bfloat16 or wider, within the bound.
A program may use at most 128 MiB of HBM per device.

v0:
```python
import jax
import jax.numpy as jnp
from jax import lax
from jax.sharding import Mesh
from jax.sharding import PartitionSpec as P

SEQ = ("seq_0", "seq_1")


epsilon = 1e-06


def from_behind(value, axis, steps):
    count = lax.axis_size(axis)
    leading, last = max(0, -steps), min(count, count - steps)
    return lax.ppermute(value, axis, [(source, source + steps) for source in range(leading, last)])


def whole_of(shard, axes, dim):
    for axis in reversed(axes):
        shard = lax.all_gather(shard, axis, axis=dim, tiled=True)
    return shard


def folded(shard, axis, dim, absorb, state):
    everything = jax.tree.map(lambda a: lax.all_gather(a, axis, axis=dim, tiled=True), shard)
    return absorb(state, everything, jnp.int32(0))


def rms_norm(values, gain):
    wide = values.astype(jnp.float32)
    factor = lax.rsqrt(jnp.mean(wide * wide, axis=-1, keepdims=True) + epsilon)
    return (wide * factor * gain).astype(jnp.bfloat16)


def block_gates(values, weight, bias):
    heads, width = (weight.shape[0], weight.shape[1])
    grouped = values.reshape(values.shape[0], heads, width)
    mixed = jnp.einsum("thi,hij->thj", grouped, weight, preferred_element_type=jnp.float32)
    return jax.nn.sigmoid(mixed.reshape(values.shape[0], heads * width) + bias)


def smooth(inner, tail, conv_weight, conv_bias):
    taps = conv_weight.shape[0]
    length = inner.shape[0]
    padded = jnp.concatenate([tail, inner], axis=0).astype(jnp.float32)
    total = conv_bias + jnp.zeros((length, inner.shape[1]), jnp.float32)
    for offset in range(taps):
        total = total + conv_weight[offset] * padded[taps - 1 - offset : taps - 1 - offset + length]
    return lax.optimization_barrier(total.astype(jnp.bfloat16))


def combine_state(earlier, later):
    return (earlier[0] * later[0], later[0] * earlier[1] + later[1])


def channel_total(partial_value):
    return lax.psum(partial_value.astype(jnp.bfloat16), "tp").astype(jnp.float32)


def on_device(
    residual,
    mix_gain,
    in_proj,
    branch_proj,
    conv_weight,
    conv_bias,
    input_gate,
    input_bias,
    decay_gate,
    decay_bias,
    decay_param,
    out_proj,
    mlp_gain,
    gate_proj,
    up_proj,
    down_proj,
):
    length = residual.shape[0]
    taps = conv_weight.shape[0]
    normed = rms_norm(residual, mix_gain)
    branch = jax.nn.gelu(
        jnp.dot(normed, branch_proj, preferred_element_type=jnp.float32), approximate=True
    )
    inner = jnp.dot(normed, in_proj, preferred_element_type=jnp.float32).astype(jnp.bfloat16)
    tail = from_behind(inner[length - (taps - 1) :], SEQ, 1)
    smoothed = smooth(inner, tail, conv_weight, conv_bias)
    input_rate = block_gates(smoothed, input_gate, input_bias)
    decay_rate = block_gates(smoothed, decay_gate, decay_bias)
    log_decay = -8.0 * decay_rate * jax.nn.softplus(decay_param)
    decay = jnp.exp(log_decay)
    position = lax.axis_index(SEQ)
    first = jnp.logical_and(position == 0, jnp.arange(length) == 0)[:, None]
    scale_in = jnp.where(first, 1.0, jnp.sqrt(-jnp.expm1(2.0 * log_decay)))
    pushed = smoothed.astype(jnp.float32) * input_rate * scale_in
    decays, partial_states = lax.associative_scan(combine_state, (decay, pushed), axis=0)
    end_decay = decays[-1]
    end_state = partial_states[-1]
    summaries = whole_of(jnp.stack([end_decay, end_state])[None], SEQ, 0)

    def fold(index, state):
        moved = summaries[index, 0] * state + summaries[index, 1]
        return jnp.where(index < position, moved, state)

    carried = lax.fori_loop(0, summaries.shape[0], fold, jnp.zeros_like(end_state))
    states = partial_states + decays * carried[None]
    gated = (states * branch).astype(jnp.bfloat16)
    mixed = channel_total(jnp.dot(gated, out_proj, preferred_element_type=jnp.float32))
    middle = lax.optimization_barrier((residual.astype(jnp.float32) + mixed).astype(jnp.bfloat16))
    hidden_in = rms_norm(middle, mlp_gain)
    width = gate_proj.shape[1]
    empty = jnp.zeros((length, width), jnp.float32)

    def add_rows(totals, pieces, start):
        columns = lax.dynamic_slice_in_dim(hidden_in, start, pieces[0].shape[0], 1)
        return (
            totals[0] + jnp.dot(columns, pieces[0], preferred_element_type=jnp.float32),
            totals[1] + jnp.dot(columns, pieces[1], preferred_element_type=jnp.float32),
        )

    gate, up = folded((gate_proj, up_proj), SEQ, 0, add_rows, (empty, empty))
    hidden = (jax.nn.gelu(gate, approximate=True) * up).astype(jnp.bfloat16)
    output = channel_total(jnp.dot(hidden, down_proj, preferred_element_type=jnp.float32))
    return (middle.astype(jnp.float32) + output).astype(jnp.bfloat16)


def solution(mesh):
    split = Mesh(mesh.devices.reshape(mesh.shape["tp"], 4, 2), ("tp", "seq_0", "seq_1"))
    in_specs = (
        P(SEQ, None),
        P(),
        P(None, "tp"),
        P(None, "tp"),
        P(None, "tp"),
        P("tp"),
        P("tp", None, None),
        P("tp"),
        P("tp", None, None),
        P("tp"),
        P("tp"),
        P("tp", None),
        P(),
        P(SEQ, "tp"),
        P(SEQ, "tp"),
        P("tp", None),
    )
    out_specs = P(SEQ, None)
    return jax.shard_map(
        on_device, mesh=split, in_specs=in_specs, out_specs=out_specs, check_vma=False
    )
```

profile of v0, /device:TPU:1, one launch (start us, length us, event | category | flops | bytes accessed | tf_op | source)
XLA Modules:
  0.0 403.9 jit_solution(9161906247059077176)
XLA Ops:
  7.4 0.0 copy-start
  7.4 0.0 all-reduce.35.cloned.1.call-start
  7.4 0.0 copy-start.2
  7.4 2.2 fusion
  9.6 0.1 copy-done.2
  9.7 0.0 copy-start.4
  9.7 0.0 copy-start.5
  9.7 0.0 copy-start.6
  9.8 0.0 copy-start.7
  9.8 0.0 copy-start.10
  9.8 2.5 convolution_convert_fusion.2
  12.3 0.0 copy-start.8
  12.3 0.0 copy-start.11
  12.3 5.6 %collective-permute-start = (bf16[3,256]{1,0:T(4,128)(2,1)S(1)}, bf16[3,256]{1,0:T(4,128)(2,1)S(1)}, u32[]{:S(2)}, u32[]{:S(2)}) collective-permute-start(bf16[3,256]{1,0:T(4,128)(2,1)S(1)} %slice.348), channel_id=1, source_target_pairs={{0,1},{1,2},{2,3},{3,4},{4,5},{5,6},{6,7},{8,9},{9,10},{10,11},{11... | collective-permute-start | bytes 4616 | tf_op jit(solution)/shard_map/ppermute | solution.py:16
  17.9 0.0 copy-done.4
  17.9 0.0 copy-done.5
  18.0 0.6 collective-permute-done
  18.6 0.0 copy-done.6
  18.7 0.1 fusion.56
  18.8 0.0 copy-done.7
  18.8 0.0 copy-done.10
  18.8 0.3 fusion.93
  19.1 0.0 copy-done.8
  19.1 0.0 copy-done.11
  19.1 0.3 fusion.19
  19.4 0.0 copy-start.3
  19.5 0.1 slice.275
  19.6 0.1 slice.276
  19.7 0.1 slice.274
  19.8 0.1 slice.278
  20.9 0.2 slice.330
  21.2 0.2 slice.273
  21.4 0.0 copy-done.3
  22.1 0.0 slice-start
  22.4 0.1 fusion.64
  22.5 0.3 slice-done
  22.9 4.9 %all-gather.1 = f32[2,2,256]{2,1,0:T(2,128)S(1)} all-gather(f32[1,2,256]{2,1,0:T(2,128)S(1)} %maximum_bitcast_fusion), channel_id=2, replica_groups=mesh['tp'=16,'seq_0'=4,'seq_1'=2] {'seq_1'}, dimensions={0}, use_global_device_ids=true | all-gather | bytes 6144 | tf_op jit(solution)/shard_map/all_gather | solution.py:21
  27.8 10.6 %all_gather.13 = f32[8,2,256]{2,1,0:T(2,128)S(1)} all-gather(f32[2,2,256]{2,1,0:T(2,128)S(1)} %all-gather.1), channel_id=1, replica_groups=mesh['tp'=16,'seq_0'=4,'seq_1'=2] {'seq_0'}, dimensions={0}, use_global_device_ids=true | all-gather | bytes 20480 | tf_op jit(solution)/shard_map/all_gather | solution.py:21
  38.4 0.4 while.14
  38.8 0.0 copy-done
  38.8 6.0 %convolution_convert_fusion = bf16[256,4096]{1,0:T(8,128)(2,1)} fusion(bf16[256,4096]{1,0:T(8,128)(2,1)S(1)} %copy-done, bf16[4096,256]{1,0:T(8,128)(2,1)} %param.21, bf16[256,4096]{1,0:T(8,128)(2,1)} %param.18, f32[4096]{0:T(1024)} %param.19, f32[256]{0:T(256)S(1)} %add_rsqrt_fusion.1, f32[256,256]{1,0:T(8,128)S(1)} %pad.128, f32[256,256]{1,0:T(8,128)S(1)} %pad.129, ...), kind=kOutput, calls=%fused_computation.9 | convolution fusion | flops 1079902208 | bytes 9455616 | tf_op jit(solution)/shard_map/dot_general | solution.py:108
  44.9 0.0 all-reduce.35.cloned.1.call-update
  44.9 0.0 all-gather.5.cloned.1.call-start
  44.9 0.5 all-gather.5.cloned.1.call-update
  45.5 0.0 all-gather.7.cloned.1.call-start
  45.5 0.5 all-gather.7.cloned.1.call-update
  46.1 0.2 all-reduce.37.cloned.1.call-start
  46.3 198.6 %all-reduce.35.cloned.1.call-done = bf16[256,4096]{1,0:T(8,128)(2,1)} async-done(((bf16[256,4096]{1,0:T(8,128)(2,1)}), bf16[256,4096]{1,0:T(8,128)(2,1)}) %all-reduce.35.cloned.1.call-update) | async-done | bytes 2097168 | tf_op jit(solution)/shard_map/psum | solution.py:58
  244.9 3.0 fusion.3
  247.9 0.0 copy-start.1
  247.9 1.3 copy-done.1
  249.2 0.0 copy-start.9
  249.2 0.5 fusion.4
  249.7 0.0 all-gather.5.cloned.1.call-done
  249.8 0.2 copy-done.9
  250.0 5.3 %fusion.29 = f32[256,768]{1,0:T(8,128)S(1)} fusion(bf16[4096,768]{1,0:T(8,128)(2,1)} %all-gather.5.cloned.1.call-done, bf16[256,4096]{1,0:T(8,128)(2,1)} %copy-done.1, f32[4096]{0:T(1024)S(1)} %copy-done.9, f32[256]{0:T(256)S(1)} %add_rsqrt_fusion), kind=kOutput, calls=%fused_computation.43 | convolution fusion | flops 1614807040 | bytes 9192448 | tf_op jit(solution)/shard_map/dot_general | solution.py:117
  255.2 0.0 all-gather.7.cloned.1.call-done
  255.3 11.3 %convolution_convert_fusion.1 = bf16[256,4096]{1,0:T(8,128)(2,1)} fusion(bf16[768,4096]{1,0:T(8,128)(2,1)} %param.33, bf16[4096,768]{1,0:T(8,128)(2,1)} %all-gather.7.cloned.1.call-done, f32[256,768]{1,0:T(8,128)S(1)} %fusion.29, bf16[256,4096]{1,0:T(8,128)(2,1)} %copy-done.1, f32[4096]{0:T(1024)S(1)} %copy-done.9, f32[256]{0:T(256)S(1)} %add_rsqrt_fusion), kind=kOutput, calls=%fused_computation.10 | convolution fusion | flops 3228434432 | bytes 17581056 | tf_op jit(solution)/shard_map/dot_general | solution.py:123
  266.5 0.0 all-reduce.37.cloned.1.call-update
  266.5 125.6 %all-reduce.37.cloned.1.call-done = bf16[256,4096]{1,0:T(8,128)(2,1)} async-done(((bf16[256,4096]{1,0:T(8,128)(2,1)}), bf16[256,4096]{1,0:T(8,128)(2,1)}) %all-reduce.37.cloned.1.call-update) | async-done | bytes 2097168 | tf_op jit(solution)/shard_map/psum | solution.py:58
  392.2 4.3 %fusion.7 = bf16[256,4096]{1,0:T(8,128)(2,1)} fusion(bf16[256,4096]{1,0:T(8,128)(2,1)} %copy-done.1, bf16[256,4096]{1,0:T(8,128)(2,1)} %all-reduce.37.cloned.1.call-done), kind=kLoop, calls=%fused_computation.18 | loop fusion | flops 4194304 | bytes 6291456 | tf_op jit(solution)/shard_map/convert_element_type | solution.py:124
  (140 shorter events, 1.9 us)
Async XLA Ops:
  7.4 31.5 %copy-start = (bf16[256,4096]{1,0:T(8,128)(2,1)S(1)}, bf16[256,4096]{1,0:T(8,128)(2,1)}, u32[]{:S(2)}) copy-start(bf16[256,4096]{1,0:T(8,128)(2,1)} %param.29) | copy-start | bytes 6291460
  7.4 237.5 %all-reduce.35.cloned.1.call-start = ((), (), s32[]{:S(2)}) async-start(), calls=%async_computation | async-start | bytes 4194304 | tf_op jit(solution)/shard_map/psum | solution.py:58
  7.4 2.4 copy-start.2
  9.7 8.2 %copy-start.4 = (f32[4,256]{1,0:T(4,128)S(1)}, f32[4,256]{1,0:T(4,128)}, u32[]{:S(2)}) copy-start(f32[4,256]{1,0:T(4,128)} %param.22) | copy-start | bytes 12292
  9.7 8.2 %copy-start.5 = (f32[256]{0:T(256)S(1)}, f32[256]{0:T(256)}, u32[]{:S(2)}) copy-start(f32[256]{0:T(256)} %param.28) | copy-start | bytes 3076
  9.7 8.9 %copy-start.6 = (f32[256]{0:T(256)S(1)}, f32[256]{0:T(256)}, u32[]{:S(2)}) copy-start(f32[256]{0:T(256)} %param.23) | copy-start | bytes 3076
  9.8 9.0 %copy-start.7 = (bf16[1,256,256]{2,1,0:T(8,128)(2,1)S(1)}, bf16[1,256,256]{2,1,0:T(8,128)(2,1)}, u32[]{:S(2)}) copy-start(bf16[1,256,256]{2,1,0:T(8,128)(2,1)} %param.26) | copy-start | bytes 393220
  9.8 9.0 %copy-start.10 = (f32[256]{0:T(256)S(1)}, f32[256]{0:T(256)}, u32[]{:S(2)}) copy-start(f32[256]{0:T(256)} %param.27) | copy-start | bytes 3076
  12.3 6.8 %copy-start.8 = (bf16[1,256,256]{2,1,0:T(8,128)(2,1)S(1)}, bf16[1,256,256]{2,1,0:T(8,128)(2,1)}, u32[]{:S(2)}) copy-start(bf16[1,256,256]{2,1,0:T(8,128)(2,1)} %param.24) | copy-start | bytes 393220
  12.3 6.8 %copy-start.11 = (f32[256]{0:T(256)S(1)}, f32[256]{0:T(256)}, u32[]{:S(2)}) copy-start(f32[256]{0:T(256)} %param.25) | copy-start | bytes 3076
  12.3 6.3 %collective-permute-start = (bf16[3,256]{1,0:T(4,128)(2,1)S(1)}, bf16[3,256]{1,0:T(4,128)(2,1)S(1)}, u32[]{:S(2)}, u32[]{:S(2)}) collective-permute-start(bf16[3,256]{1,0:T(4,128)(2,1)S(1)} %slice.348), channel_id=1, source_target_pairs={{0,1},{1,2},{2,3},{3,4},{4,5},{5,6},{6,7},{8,9},{9,10},{10,11},{11... | collective-permute-start | bytes 4616 | tf_op jit(solution)/shard_map/ppermute | solution.py:16
  19.4 2.0 copy-start.3
  22.1 0.7 slice-start
  44.9 204.9 %all-gather.5.cloned.1.call-start = ((), (), s32[]{:S(2)}) async-start(), calls=%async_computation.1 | async-start | bytes 7077888 | tf_op jit(solution)/shard_map/all_gather | solution.py:26
  45.5 209.8 %all-gather.7.cloned.1.call-start = ((), (), s32[]{:S(2)}) async-start(), calls=%async_computation.2 | async-start | bytes 7077888 | tf_op jit(solution)/shard_map/all_gather | solution.py:26
  46.1 346.1 %all-reduce.37.cloned.1.call-start = ((), (), s32[]{:S(2)}) async-start(), calls=%async_computation.3 | async-start | bytes 4194304 | tf_op jit(solution)/shard_map/psum | solution.py:58
  247.9 1.3 copy-start.1
  249.2 0.7 copy-start.9
Sparse Core Ops, SparseCore 0:
  45.0 199.8 all-reduce.34
  266.7 125.4 all-reduce.36
Sparse Core Ops, SparseCore 1:
  47.7 93.5 all-gather.4
  143.4 85.6 all-gather.6
where the time goes:
time: 404 us
  waiting for transfers between devices  326 us (81%)
  matrix products  25.6 us (6%)
  between operations  15.8 us (4%)
  blocking collectives  15.5 us (4%)
  other arithmetic  10.9 us (3%)
  starting transfers between devices  5.89 us (1%)
  local copies, waits for them, and re-layouts  4.04 us (1%)
    psum x2, waiting for transfers between devices, channel_total(): lax.psum(partial_value.astype(jnp.bfloat16), 'tp').astype(jnp.float32)  324 us
    all_gather x2, blocking collectives, whole_of(): shard = lax.all_gather(shard, axis, axis=dim, tiled=True)  15.5 us
    dot_general x1, matrix products, on_device(): jnp.dot(hidden, down_proj, preferred_element_type=jnp.float32)  11.3 us
  transfers between devices with their start and end apart: 5, of which 3 were waited for; matrix products, arithmetic and copies ran while one was open for 2% of the time, Pallas kernels for 0%

commit v1 on v0

v1 whole, which is shorter than its diff:
```python
import math

import jax
import jax.numpy as jnp
from jax import lax
from jax.experimental import pallas as pl
from jax.experimental.pallas import tpu as pltpu
from jax.sharding import Mesh
from jax.sharding import PartitionSpec as P

SEQ = ("y", "x_hi")
TP = ("x_lo", "z", "core")
AXES = ("x_lo", "z", "core", "y", "x_hi")
BF = jnp.bfloat16
F32 = jnp.float32
EPS = 1e-06

ROWS = 256
D = 4096
HALF = D // 2
WIDTH = 256
FF = 768
PIECE = 16
CHUNK = 256
CHUNKS = FF // CHUNK
DEPTH = 512
SLOTS = 96


def gelu(v):
    return 0.5 * v * (1.0 + jnp.tanh(math.sqrt(2.0 / math.pi) * (v + 0.044715 * v * v * v)))


def one_less_exp(v):
    series = 1.0 + v / 8.0
    for n in (7.0, 6.0, 5.0, 4.0, 3.0, 2.0):
        series = 1.0 + v / n * series
    return jnp.where(v > -0.25, -v * series, 1.0 - jnp.exp(v))


def softplus(v):
    t = jnp.exp(-jnp.abs(v))
    series = 1.0 / 7.0 - t / 8.0
    for n in (6.0, 5.0, 4.0, 3.0, 2.0, 1.0):
        series = 1.0 / n - t * series
    return jnp.maximum(v, 0.0) + jnp.where(t < 0.05, t * series, jnp.log(1.0 + t))


def kernel(
    residual_h, mix_gain, in_h, branch_h, conv_w, conv_b, input_gate, input_bias, decay_gate, decay_bias,
    decay_param, out_proj_h, mlp_gain, gate_h, up_h, down_h,
    updated,
    res, w_in, w_branch, w_out, w_down, w_gate, w_up,
    normed, inner, branch, tail, pad, decays, states, sum_out, sums, gated,
    part, near, halved, xa, s2a, za, zb, s2b, xb,
    middle, hid_out, hid, gate_out, up_out, gate_mid, up_mid, gate_in, up_in, gate_own, up_own, hidden, final,
    loc, send, recv,
):
    x_lo, z, core, y, x_hi = (lax.axis_index(a) for a in AXES)
    position = y * 2 + x_hi
    x = x_hi * 2 + x_lo

    def at_x(step):
        there = lax.rem(x + step, 4)
        return {"x_hi": there // 2, "x_lo": lax.rem(there, 2)}

    def at_y(step):
        return {"y": lax.rem(y + step, 4)}

    def at_z(step):
        return {"z": lax.rem(z + step, 4)}

    def at_seq(step):
        there = lax.rem(position + step, 8)
        return {"y": there // 2, "x_hi": lax.rem(there, 2)}

    at_core = {"core": 1 - core}
    at_pair = {"x_lo": 1 - x_lo}
    at_hi = {"x_hi": 1 - x_hi}

    used = [0]
    started = []

    def remote(src, dst, where):
        n = used[0]
        used[0] += 1
        return pltpu.make_async_remote_copy(
            src_ref=src, dst_ref=dst, send_sem=send.at[n], recv_sem=recv.at[n],
            device_id=where, device_id_type=pl.DeviceIdType.MESH,
        )

    def go(*copies):
        for copy in copies:
            copy.start()
            started.append(copy)

    def local(n, src, dst):
        copy = pltpu.make_async_copy(src, dst, loc.at[n])
        copy.start()
        return copy

    my_rows = pl.ds(pl.multiple_of(y * DEPTH, DEPTH), DEPTH)
    load_res = local(0, residual_h, res)
    load_in = local(1, in_h, w_in)
    load_branch = local(2, branch_h, w_branch)

    barrier = pltpu.get_barrier_semaphore()
    partners = [at_core, at_x(1), at_x(3), at_z(1), at_z(2), at_z(3)] + [at_seq(s) for s in range(1, 8)]
    for where in partners:
        pl.semaphore_signal(barrier, inc=1, device_id=where, device_id_type=pl.DeviceIdType.MESH)

    load_res.wait()

    @pl.loop(0, ROWS // PIECE)
    def _(i):
        rows = pl.ds(pl.multiple_of(i * PIECE, PIECE), PIECE)
        wide = res[rows, :].astype(F32)
        factor = lax.rsqrt(jnp.mean(wide * wide, axis=-1, keepdims=True) + EPS)
        normed[rows, :] = (wide * factor * mix_gain[...]).astype(BF)

    pl.semaphore_wait(barrier, len(partners))

    up_y, down_y = at_y(1), at_y(3)
    back = [pl.ds(pl.multiple_of(lax.rem(y + s, 4) * DEPTH, DEPTH), DEPTH) for s in range(4)]
    cols = [pl.ds(c * CHUNK, CHUNK) for c in range(CHUNKS)]
    own_gate_up = [remote(gate_h.at[:, cols[c]], w_gate.at[my_rows, cols[c]], up_y) for c in range(CHUNKS)]
    own_up_up = [remote(up_h.at[:, cols[c]], w_up.at[my_rows, cols[c]], up_y) for c in range(CHUNKS)]
    own_gate_down = [remote(gate_h.at[:, cols[c]], w_gate.at[my_rows, cols[c]], down_y) for c in range(CHUNKS)]
    own_up_down = [remote(up_h.at[:, cols[c]], w_up.at[my_rows, cols[c]], down_y) for c in range(CHUNKS)]
    pass_gate = [
        remote(w_gate.at[back[3], cols[c]], w_gate.at[back[3], cols[c]], up_y) for c in range(CHUNKS)
    ]
    pass_up = [remote(w_up.at[back[1], cols[c]], w_up.at[back[1], cols[c]], down_y) for c in range(CHUNKS)]

    go(own_gate_up[0], own_up_down[0])

    load_gate = local(5, gate_h, w_gate.at[my_rows, :])
    load_up = local(6, up_h, w_up.at[my_rows, :])
    load_out = local(3, out_proj_h, w_out)
    load_down = local(4, down_h, w_down)

    load_in.wait()
    inner_f32 = jnp.dot(normed[...], w_in[...], preferred_element_type=F32).astype(BF)
    inner[...] = inner_f32
    send_tail = remote(inner.at[pl.ds(ROWS - 16, 16), :], tail, at_seq(1))
    go(send_tail)
    pad[pl.ds(8, ROWS), :] = inner_f32.astype(F32)
    go(own_up_up[0], own_gate_down[0])

    load_branch.wait()
    branch[...] = gelu(jnp.dot(normed[...], w_branch[...], preferred_element_type=F32))

    send_tail.wait_recv()
    before = tail[...].astype(F32)[8:16, :]
    pad[pl.ds(0, 8), :] = jnp.where(position == 0, 0.0, before)

    total = conv_b[...] + jnp.zeros((ROWS, WIDTH), F32)
    for k in range(4):
        total = total + conv_w[pl.ds(k, 1), :] * pad[pl.ds(8 - k, ROWS), :]
    smoothed = total.astype(BF)
    input_rate = jax.nn.sigmoid(
        jnp.dot(smoothed, input_gate[0], preferred_element_type=F32) + input_bias[...]
    )
    decay_rate = jax.nn.sigmoid(
        jnp.dot(smoothed, decay_gate[0], preferred_element_type=F32) + decay_bias[...]
    )
    log_decay = -8.0 * decay_rate * softplus(decay_param[...])
    row = lax.broadcasted_iota(jnp.int32, (ROWS, WIDTH), 0)
    scale_in = jnp.sqrt(one_less_exp(2.0 * log_decay))
    scale_in = jnp.where(jnp.logical_and(row == 0, position == 0), 1.0, scale_in)
    a = jnp.exp(log_decay)
    b = smoothed.astype(F32) * input_rate * scale_in
    step = 1
    while step < ROWS:
        a_before = jnp.where(row < step, 1.0, pltpu.roll(a, step, 0))
        b_before = jnp.where(row < step, 0.0, pltpu.roll(b, step, 0))
        b = a * b_before + b
        a = a * a_before
        step *= 2
    decays[...] = a
    states[...] = b
    sum_out[...] = jnp.zeros((8, WIDTH), F32)
    sum_out[pl.ds(0, 1), :] = a[ROWS - 1 :, :]
    sum_out[pl.ds(1, 1), :] = b[ROWS - 1 :, :]
    send_sums = [remote(sum_out, sums.at[s], at_seq(s)) for s in range(1, 8)]
    go(*send_sums)

    own_gate_up[0].wait_recv()
    own_up_down[0].wait_recv()
    go(pass_gate[0], pass_up[0])
    go(own_gate_up[1], own_up_down[1], own_up_up[1], own_gate_down[1])

    for copy in send_sums:
        copy.wait_recv()
    carried = jnp.zeros((1, WIDTH), F32)
    for s in range(7, 0, -1):
        moved = sums[s, pl.ds(0, 1), :] * carried + sums[s, pl.ds(1, 1), :]
        carried = jnp.where(position >= s, moved, carried)
    gated[...] = ((states[...] + decays[...] * carried) * branch[...]).astype(BF)

    first, second = pl.ds(0, HALF), pl.ds(HALF, HALF)

    def partial_products(turn, lhs, weights, base):
        @pl.loop(0, HALF // 512)
        def _(i):
            columns = pl.ds(pl.multiple_of(base + i * 512, 512), 512)
            product = jnp.dot(lhs[...], weights[:, columns], preferred_element_type=F32)
            part[turn, :, :, :, :, columns] = product.astype(BF).reshape(2, 2, 4, PIECE, 512)

    def sum_over_tp(turn, lhs, weights, between):
        there = 1 - core
        swap = []
        for half in (first, second):
            partial_products(turn, lhs, weights, 0 if half is first else HALF)
            copy = remote(part.at[turn, there, :, :, :, half], near.at[turn, :, :, :, half], at_core)
            go(copy)
            swap.append(copy)

        def add_near(half):
            @pl.loop(0, 8)
            def _(i):
                xl, zz = i // 4, lax.rem(i, 4)
                halved[turn, xl, zz, :, half] = (
                    part[turn, core, xl, zz, :, half].astype(F32) + near[turn, xl, zz, :, half].astype(F32)
                ).astype(BF)

        swap[0].wait_recv()
        add_near(first)
        across = remote(halved.at[turn, 1 - x_lo, :, :, first], xa.at[turn], at_pair)
        go(across)
        swap[1].wait_recv()
        add_near(second)
        around = [
            remote(halved.at[turn, :, lax.rem(z + s, 4), :, second], zb.at[turn, s - 1], at_z(s))
            for s in (1, 3, 2)
        ]
        go(*around)
        between()
        across.wait_recv()

        @pl.loop(0, 4)
        def _(i):
            s2a[turn, i] = (
                halved[turn, x_lo, i, :, first].astype(F32) + xa[turn, i].astype(F32)
            ).astype(BF)

        around_a = [
            remote(s2a.at[turn, lax.rem(z + s, 4)], za.at[turn, s - 1], at_z(s)) for s in (1, 3, 2)
        ]
        go(*around_a)
        for copy in around:
            copy.wait_recv()

        @pl.loop(0, 2)
        def _(i):
            whole = halved[turn, i, z, :, second].astype(F32)
            for s in range(3):
                whole = whole + zb[turn, s, i].astype(F32)
            s2b[turn, i] = whole.astype(BF)

        across_b = remote(s2b.at[turn, 1 - x_lo], xb.at[turn], at_pair)
        go(across_b)
        for copy in around_a:
            copy.wait_recv()
        left = s2a[turn, z].astype(F32)
        for s in range(3):
            left = left + za[turn, s].astype(F32)
        across_b.wait_recv()
        right = s2b[turn, x_lo].astype(F32) + xb[turn].astype(F32)
        return left, right

    load_out.wait()

    def pass_second():
        own_gate_up[1].wait_recv()
        own_up_down[1].wait_recv()
        go(pass_gate[1], pass_up[1])
        go(own_gate_up[2], own_up_down[2], own_up_up[2], own_gate_down[2])

    left, right = sum_over_tp(0, gated, w_out, pass_second)
    mine = pl.ds(pl.multiple_of(core * 128 + x_lo * 64 + z * PIECE, PIECE), PIECE)
    middle[:, first] = (res[mine, first].astype(F32) + left).astype(BF)
    middle[:, second] = (res[mine, second].astype(F32) + right).astype(BF)
    wide = middle[...].astype(F32)
    factor = lax.rsqrt(jnp.mean(wide * wide, axis=-1, keepdims=True) + EPS)
    wide = (wide * factor * mlp_gain[...]).astype(BF)

    for i in range(4):
        even = wide[:, 2 * i * DEPTH : (2 * i + 1) * DEPTH]
        odd = wide[:, (2 * i + 1) * DEPTH : (2 * i + 2) * DEPTH]
        block = pl.ds(i * DEPTH, DEPTH)
        hid[x_hi, core, x_lo, z, :, block] = jnp.where(x_hi == 0, even, odd)
        hid_out[:, block] = jnp.where(x_hi == 0, odd, even)

    def gather_over_tp(own_a, own_b, enter):
        z_a = [remote(own_a(core, x_lo, z), own_a(core, x_lo, z), at_z(s)) for s in (1, 3, 2)]
        go(*z_a)
        enter()
        x_b = remote(own_b(core, x_lo, z), own_b(core, x_lo, z), at_pair)
        go(x_b)
        for copy in z_a:
            copy.wait_recv()
        everything = slice(None)
        x_a = remote(own_a(core, x_lo, everything), own_a(core, x_lo, everything), at_pair)
        c_a = remote(own_a(core, x_lo, everything), own_a(core, x_lo, everything), at_core)
        go(x_a, c_a)
        x_b.wait_recv()
        z_b = [remote(own_b(core, everything, z), own_b(core, everything, z), at_z(s)) for s in (1, 3, 2)]
        go(*z_b)
        x_a.wait_recv()
        c_a2 = remote(own_a(core, 1 - x_lo, everything), own_a(core, 1 - x_lo, everything), at_core)
        go(c_a2)
        for copy in z_b:
            copy.wait_recv()
        c_b = remote(own_b(core, everything, everything), own_b(core, everything, everything), at_core)
        go(c_b)
        return c_a, c_a2, c_b

    to_hi = remote(hid_out, hid.at[x_hi, core, x_lo, z], at_hi)
    go(to_hi)
    last = gather_over_tp(
        lambda c, l, k: hid.at[x_hi, c, l, k],
        lambda c, l, k: hid.at[1 - x_hi, c, l, k],
        to_hi.wait_recv,
    )
    own_gate_up[2].wait_recv()
    own_up_down[2].wait_recv()
    go(pass_gate[2], pass_up[2])
    for copy in last:
        copy.wait_recv()

    load_gate.wait()
    load_up.wait()
    gate_hop, up_hop, gate_last, up_last = [], [], [], []
    for c in range(CHUNKS):
        gate_hop.append(remote(gate_out.at[c], gate_mid.at[c], at_x(1)))
        up_hop.append(remote(up_out.at[c], up_mid.at[c], at_x(3)))
        gate_last.append(remote(gate_mid.at[c], gate_in.at[c], at_x(1)))
        up_last.append(remote(up_mid.at[c], up_in.at[c], at_x(3)))

    def features(group, weights, c):
        lhs = hid[group].reshape(ROWS, HALF)
        return jnp.dot(lhs, weights[:, cols[c]], preferred_element_type=F32)

    for c in range(CHUNKS):
        for copy in (own_up_up[c], own_gate_down[c], pass_gate[c], pass_up[c]):
            copy.wait_recv()
        gate_out[c] = features(1 - x_hi, w_gate, c).astype(BF)
        go(gate_hop[c])
        up_out[c] = features(1 - x_hi, w_up, c).astype(BF)
        go(up_hop[c])
        gate_own[:, cols[c]] = features(x_hi, w_gate, c)
        up_own[:, cols[c]] = features(x_hi, w_up, c)
    for c in range(CHUNKS):
        gate_hop[c].wait_recv()
        up_hop[c].wait_recv()
        go(gate_last[c], up_last[c])
    for c in range(CHUNKS):
        gate_last[c].wait_recv()
        up_last[c].wait_recv()
        gate = gate_own[:, cols[c]] + gate_in[c].astype(F32)
        up = up_own[:, cols[c]] + up_in[c].astype(F32)
        hidden[:, cols[c]] = (gelu(gate) * up).astype(BF)

    load_down.wait()
    left, right = sum_over_tp(1, hidden, w_down, lambda: None)
    final[core, x_lo, z, :, first] = (middle[:, first].astype(F32) + left).astype(BF)
    final[core, x_lo, z, :, second] = (middle[:, second].astype(F32) + right).astype(BF)
    last = gather_over_tp(
        lambda c, l, k: final.at[c, l, k, :, first] if not isinstance(k, slice) else final.at[c, l, :, :, first],
        lambda c, l, k: (
            final.at[c, l, k, :, second]
            if not isinstance(l, slice)
            else (final.at[c, :, k, :, second] if not isinstance(k, slice) else final.at[c, :, :, :, second])
        ),
        lambda: None,
    )
    stores = [local(7, final.at[core], updated.at[core])]
    for copy in last:
        copy.wait_recv()
    stores.append(local(8, final.at[1 - core], updated.at[1 - core]))
    for copy in stores:
        copy.wait()
    for copy in started:
        copy.wait_send()


def on_device(*args):
    vmem = pl.BlockSpec(memory_space=pltpu.VMEM)
    hbm = pl.BlockSpec(memory_space=pl.ANY)
    places = [hbm, vmem, hbm, hbm, vmem, vmem, vmem, vmem, vmem, vmem, vmem, hbm, vmem, hbm, hbm, hbm]
    args = [a.reshape(1, -1) if a.ndim == 1 else a for a in args]
    v = pltpu.VMEM
    scratch = [
        v((ROWS, D), BF), v((D, WIDTH), BF), v((D, WIDTH), BF), v((WIDTH, D), BF), v((FF, D), BF),
        v((4 * DEPTH, FF), BF), v((4 * DEPTH, FF), BF),
        v((ROWS, D), BF), v((ROWS, WIDTH), BF), v((ROWS, WIDTH), F32), v((16, WIDTH), BF),
        v((ROWS + 8, WIDTH), F32), v((ROWS, WIDTH), F32), v((ROWS, WIDTH), F32), v((8, WIDTH), F32),
        v((8, 8, WIDTH), F32), v((ROWS, WIDTH), BF),
        v((2, 2, 2, 4, PIECE, D), BF), v((2, 2, 4, PIECE, D), BF), v((2, 2, 4, PIECE, D), BF),
        v((2, 4, PIECE, HALF), BF), v((2, 4, PIECE, HALF), BF), v((2, 3, PIECE, HALF), BF),
        v((2, 3, 2, PIECE, HALF), BF), v((2, 2, PIECE, HALF), BF), v((2, PIECE, HALF), BF),
        v((PIECE, D), BF), v((PIECE, HALF), BF), v((2, 2, 2, 4, PIECE, HALF), BF),
        v((CHUNKS, ROWS, CHUNK), BF), v((CHUNKS, ROWS, CHUNK), BF), v((CHUNKS, ROWS, CHUNK), BF),
        v((CHUNKS, ROWS, CHUNK), BF), v((CHUNKS, ROWS, CHUNK), BF), v((CHUNKS, ROWS, CHUNK), BF),
        v((ROWS, FF), F32), v((ROWS, FF), F32), v((ROWS, FF), BF), v((2, 2, 4, PIECE, D), BF),
        pltpu.SemaphoreType.DMA((9,)), pltpu.SemaphoreType.DMA((SLOTS,)), pltpu.SemaphoreType.DMA((SLOTS,)),
    ]
    out = pl.pallas_call(
        kernel,
        name="layer",
        out_shape=jax.ShapeDtypeStruct((2, 2, 4, PIECE, D), BF),
        in_specs=places,
        out_specs=hbm,
        scratch_shapes=scratch,
        compiler_params=pltpu.CompilerParams(
            collective_id=0, has_side_effects=True, vmem_limit_bytes=60 * 1024 * 1024
        ),
    )(*args)
    return out.reshape(ROWS, D)


def solution(mesh):
    split = Mesh(mesh.devices.reshape(2, 4, 2, 4, 2), AXES)
    in_specs = (
        P(SEQ, None), P(), P(None, TP), P(None, TP), P(None, TP), P(TP), P(TP, None, None), P(TP),
        P(TP, None, None), P(TP), P(TP), P(TP, None), P(), P(SEQ, TP), P(SEQ, TP), P(TP, None),
    )
    return jax.shard_map(
        on_device, mesh=split, in_specs=in_specs, out_specs=P(SEQ, None), check_vma=False
    )
```

time: 404 us -> 114 us (0.28)
  waiting for transfers between devices: 326 us -> 0 us
  Pallas kernels: 0 us -> 111 us
  matrix products: 25.6 us -> 0 us
  between operations: 15.8 us -> 0.01 us
  blocking collectives: 15.5 us -> 0 us
  other arithmetic: 10.9 us -> 0 us
  starting transfers between devices: 5.89 us -> 0 us
    psum x2 -> x0, waiting for transfers between devices: 324 us -> none  [channel_total(): lax.psum(partial_value.astype(jnp.bfloat16), 'tp').astype(jnp.float32)]
    pallas_call x0 -> x1, Pallas kernels: none -> 111 us  [on_device(): pl.pallas_call(kernel, name='layer', out_shape=jax.ShapeDtypeStruct((2, 2...]
    dot_general x6 -> x0, matrix products: 25.6 us -> none  [the longest x1 11.3 us: on_device(): jnp.dot(hidden, down_proj, preferred_element_type=jnp.float32)]
    all_gather x2 -> x0, blocking collectives: 15.5 us -> none  [whole_of(): shard = lax.all_gather(shard, axis, axis=dim, tiled=True)]
    convert_element_type x4 -> x0, other arithmetic: 7.49 us -> none  [the longest x1 4.32 us: on_device(): return (middle.astype(jnp.float32) + output).astype(jnp.bfloat16)]
    ppermute x1 -> x0, starting transfers between devices: 5.59 us -> none  [from_behind(): lax.ppermute(value, axis, [(source, source + steps) for source in range(l...]
  transfers between devices with their start and end apart: 5 -> 0, of which waited for: 3 -> 0; matrix products, arithmetic and copies ran while one was open for 2% -> 0% of each run, Pallas kernels for 0% -> 0%
where the time goes in v1:
time: 114 us
  Pallas kernels  111 us (97%)
  local copies, waits for them, and re-layouts  3.13 us (3%)
    pallas_call x1, Pallas kernels, on_device(): pl.pallas_call(kernel, name='layer', out_shape=jax.ShapeDtypeStruct((2, 2...  111 us
    unnamed x1, local copies, waits for them, and re-layouts  3.13 us

profile of v1, /device:TPU:1, one launch (start us, length us, event | category | flops | bytes accessed | tf_op | source)
XLA Modules:
  0.0 113.7 jit_solution(7537624946213047558)
XLA Ops:
  0.0 110.5 %layer.1 = bf16[2,2,4,16,4096]{4,3,2,1,0:T(8,128)(2,1)} custom-call(bf16[256,4096]{1,0:T(8,128)(2,1)} %residual_h.1, f32[1,4096]{1,0:T(1,128)} %bitcast.8, bf16[4096,256]{1,0:T(8,128)(2,1)} %in_h.1, bf16[4096,256]{1,0:T(8,128)(2,1)} %branch_h.1, f32[4,256]{1,0:T(4,128)} %conv_w.1, f32[1,256]{1,0:T(1,128)} %bitcast.10, bf16[1,256,256]{2,1,0:T(8,128)(2,1)} %input_gate.1, ...), custom_call_target="tpu_custom_call" | custom-call | tf_op jit(solution)/shard_map/layer/pallas_call | solution.py:409
  110.6 3.1 %copy.18 = bf16[256,4096]{1,0:T(8,128)(2,1)} copy(bf16[256,4096]{1,0:T(8,128)(2,1)} %bitcast.7) | data formatting | bytes 4194304
